TPU v7x, 512 devices: a whole 4x8x8 slice. The times are simulated.
512 devices in a mesh: seq: 128 (over y, z, core), head: 4 (over x).
Axes of the slice: x: 4, y: 8, z: 8, core: 2. Of those that a mesh axis runs over, the one named last changes fastest.
Arguments:
- hidden_states: bfloat16 [8, 8192, 3584], P(None, 'seq', 'head'), may hold values from -6 to 6
- boundary: int32 [8, 64], replicated, may hold values from 0 to 8191, as said below
- valid: int32 [8, 64], replicated, may hold values from 0 to 1, as said below
- pairs: int32 [8, 2], replicated, may hold values from 0 to 7, as said below
- w_first: bfloat16 [3584, 4096], P('seq', 'head'), may hold values from -0.09375 to 0.09375
- b_first: float32 [4096], P('head'), may hold values from -3 to 3
- w_second: float32 [4096], P('head'), may hold values from -0.09375 to 0.09375
Outputs:
- step_reward: float32 [8, 64], replicated
- trace_score: float32 [8], replicated
- margin: float32 [8], replicated
Inputs may be any that keep to these rules, and one draw needn't show every extreme that they name: Within a trace the 64 boundary positions are distinct and increasing. In each trace the ones come first; every trace has 16 to 64 valid steps. `pairs`: the two traces of a pair differ.
All inputs are finite; a program needn't handle non-finite values.
Results may differ from a plain program's by a relative error of at most 0.0003.
Values may be sent and summed in bfloat16 or wider, within the bound.
No kernel may reach another device: no remote copies, remote signals or barrier semaphores. Data moves between devices by JAX's collectives and lax.ppermute only.
A program may use at most 64 MiB of HBM per device.

v0:
```python
import jax
import jax.numpy as jnp
from jax import lax
from jax.sharding import Mesh
from jax.sharding import PartitionSpec as P

SEQ = ("seq_0", "seq_1", "seq_2")
SEQ_HEAD = ("seq_0", "seq_1", "seq_2", "head")


def laid_out(pieces, dim):
    pieces = jnp.moveaxis(pieces, 0, dim)
    shape = pieces.shape
    return pieces.reshape(*shape[:dim], shape[dim] * shape[dim + 1], *shape[dim + 2 :])


def sent_to_all(shard, axis):
    copies = jnp.broadcast_to(shard, (lax.axis_size(axis), *shard.shape))
    return lax.all_to_all(copies, axis, split_axis=0, concat_axis=0, tiled=True)


def gather_directly(shard, axis, dim):
    return laid_out(sent_to_all(shard, axis), dim)


def over_axes(shard, axes):
    for axis in axes:
        shard = lax.psum(shard, axis)
    return shard


def score_rows(rows, w_first, b_first, w_second):
    pre = jnp.dot(
        rows, lax.all_gather(w_first, SEQ, axis=0, tiled=True), preferred_element_type=jnp.float32
    )
    return jnp.sum(jnp.maximum(pre + b_first, 0.0) * w_second, axis=-1)


def per_device(hidden_states, boundary, valid, pairs, w_first, b_first, w_second):
    traces, tok_dev, quarter = hidden_states.shape
    offset = lax.axis_index(SEQ) * tok_dev
    positions = offset + jnp.arange(tok_dev, dtype=jnp.int32)
    hits = boundary[:, :, None] == positions[None, None, :]
    whole = gather_directly(hidden_states, "head", 2)
    token_logit = score_rows(
        whole.reshape(traces * tok_dev, whole.shape[2]), w_first, b_first, w_second
    )
    token_logit = token_logit.reshape(traces, tok_dev)
    partial_logit = jnp.sum(jnp.where(hits, token_logit[:, None, :], 0.0), axis=2)
    logit = over_axes(partial_logit, SEQ_HEAD)
    live = valid == 1
    step_reward = jnp.where(live, logit, jnp.float32(0.0))
    trace_score = jnp.min(jnp.where(live, logit, jnp.float32(1e30)), axis=1)
    trace_ids = jnp.arange(traces, dtype=jnp.int32)[None, :]
    winner = jnp.sum(jnp.where(pairs[:, 0:1] == trace_ids, trace_score[None, :], 0.0), axis=1)
    loser = jnp.sum(jnp.where(pairs[:, 1:2] == trace_ids, trace_score[None, :], 0.0), axis=1)
    return (step_reward, trace_score, winner - loser)


def solution(mesh):
    torus = Mesh(
        mesh.devices.reshape(8, 8, 2, mesh.shape["head"]), ("seq_0", "seq_1", "seq_2", "head")
    )
    return jax.shard_map(
        per_device,
        mesh=torus,
        in_specs=(P(None, SEQ, "head"), P(), P(), P(), P(SEQ, "head"), P("head"), P("head")),
        out_specs=(P(), P(), P()),
        check_vma=False,
    )
```

profile of v0, /device:TPU:1, one launch (start us, length us, event | category | flops | bytes accessed | tf_op | source)
XLA Modules:
  0.0 175.0 jit_solution(17195538024517947789)
XLA Ops:
  7.2 0.0 all-gather.3.cloned.1.call-start
  7.2 0.7 all-gather.3.cloned.1.call-update
  7.9 3.6 %broadcast_in_dim.47 = bf16[4,8,64,896]{3,2,1,0:T(8,128)(2,1)} broadcast(bf16[8,64,896]{2,1,0:T(8,128)(2,1)} %param.7), dimensions={1,2,3} | broadcast | bytes 4587520 | tf_op jit(solution)/shard_map/broadcast_in_dim | solution.py:18
  11.5 0.0 copy-start.3
  11.5 5.0 %all-to-all-start = ((bf16[4,8,64,896]{3,2,1,0:T(8,128)(2,1)}), bf16[4,8,64,896]{3,2,1,0:T(8,128)(2,1)}, u32[]{:S(2)}, u32[]{:S(2)}) async-start(bf16[4,8,64,896]{3,2,1,0:T(8,128)(2,1)} %broadcast_in_dim.47), calls=%async_computation | async-start | bytes 7340032 | tf_op jit(solution)/shard_map/all_to_all | solution.py:19
  16.4 0.0 copy-done.3
  16.4 37.6 %all-to-all-done = bf16[4,8,64,896]{3,2,1,0:T(8,128)(2,1)} async-done(((bf16[4,8,64,896]{3,2,1,0:T(8,128)(2,1)}), bf16[4,8,64,896]{3,2,1,0:T(8,128)(2,1)}, u32[]{:S(2)}, u32[]{:S(2)}) %all-to-all-start) | async-done | bytes 3670048 | tf_op jit(solution)/shard_map/all_to_all | solution.py:19
  54.0 4.9 %copy.11 = bf16[8,64,4,896]{3,2,1,0:T(4,128)(2,1)S(1)} copy(bf16[8,64,4,896]{3,1,0,2:T(8,128)(2,1)} %bitcast) | data formatting | bytes 7340032 | tf_op jit(solution)/shard_map/transpose | solution.py:12
  58.9 2.4 %copy.12 = bf16[64,8,4,896]{3,1,2,0:T(8,128)(2,1)} copy(bf16[64,8,4,896]{3,2,1,0:T(4,128)(2,1)S(1)} %bitcast.11) | data formatting | bytes 7340032
  61.3 0.0 copy-start.4
  61.3 0.0 copy-start.5
  61.3 43.5 %all-gather.3.cloned.1.call-done = bf16[128,28,1024]{2,1,0:T(8,128)(2,1)} async-done(((bf16[1,28,1024]{2,1,0:T(8,128)(2,1)}), bf16[128,28,1024]{2,1,0:T(8,128)(2,1)}) %all-gather.3.cloned.1.call-update) | async-done | bytes 7340048 | tf_op jit(solution)/shard_map/all_gather | solution.py:34
  104.8 10.9 %reshape.16 = bf16[3584,1024]{1,0:T(8,128)(2,1)} reshape(bf16[128,28,1024]{2,1,0:T(8,128)(2,1)} %all-gather.3.cloned.1.call-done) | data formatting | bytes 14680064
  115.7 0.0 copy-done.4
  115.7 0.0 copy-done.5
  115.7 0.0 copy-start
  115.7 0.0 copy-start.1
  115.8 8.3 %multiply_reduce_fusion = f32[512]{0:T(512)S(1)} fusion(bf16[512,3584]{1,0:T(8,128)(2,1)} %bitcast.12, bf16[3584,1024]{1,0:T(8,128)(2,1)} %reshape.16, f32[1024]{0:T(1024)S(1)} %copy-done.4, f32[1024]{0:T(1024)S(1)} %copy-done.5), kind=kOutput, calls=%fused_computation | convolution fusion | flops 3760193024 | bytes 11020288 | tf_op jit(solution)/shard_map/dot_general | solution.py:33
  124.0 0.1 broadcast_in_dim.48
  124.1 0.0 copy-done
  124.1 0.3 select_reduce_fusion
  124.4 12.0 %psum.28 = f32[8,64]{1,0:T(8,128)S(1)} all-reduce(f32[8,64]{1,0:T(8,128)S(1)} %select_reduce_fusion), channel_id=1, replica_groups=mesh['seq_0'=8,'seq_1'=8,'seq_2'=2,'head'=4] {'seq_0'}, use_global_device_ids=true, to_apply=%region_2.3 | all-reduce | flops 512 | bytes 4096 | tf_op jit(solution)/shard_map/psum | solution.py:28
  136.4 12.1 %psum.29 = f32[8,64]{1,0:T(8,128)S(1)} all-reduce(f32[8,64]{1,0:T(8,128)S(1)} %psum.28), channel_id=1, replica_groups=mesh['seq_0'=8,'seq_1'=8,'seq_2'=2,'head'=4] {'seq_1'}, use_global_device_ids=true, to_apply=%region_3.4 | all-reduce | flops 512 | bytes 4096 | tf_op jit(solution)/shard_map/psum | solution.py:28
  148.5 9.8 %psum.30 = f32[8,64]{1,0:T(8,128)S(1)} all-reduce(f32[8,64]{1,0:T(8,128)S(1)} %psum.29), channel_id=1, replica_groups=mesh['seq_0'=8,'seq_1'=8,'seq_2'=2,'head'=4] {'seq_2'}, use_global_device_ids=true, to_apply=%region_4.5 | all-reduce | flops 512 | bytes 4096 | tf_op jit(solution)/shard_map/psum | solution.py:28
  158.3 8.4 %psum.31 = f32[8,64]{1,0:T(8,128)S(1)} all-reduce(f32[8,64]{1,0:T(8,128)S(1)} %psum.30), channel_id=1, replica_groups=mesh['seq_0'=8,'seq_1'=8,'seq_2'=2,'head'=4] {'head'}, use_global_device_ids=true, to_apply=%region_5.6 | all-reduce | flops 512 | bytes 4096 | tf_op jit(solution)/shard_map/psum | solution.py:28
  166.7 0.0 copy-done.1
  166.7 0.1 select_reduce_fusion.3
  166.8 0.0 copy-start.2
  166.8 0.6 broadcast_select_fusion
  167.4 0.2 select_reduce_fusion.1
  167.6 0.5 sub.3
  168.2 0.0 copy-done.2
  (2 shorter events, 0.0 us)
Async XLA Ops:
  7.2 97.6 %all-gather.3.cloned.1.call-start = ((), (), s32[]{:S(2)}) async-start(), calls=%async_computation.1 | async-start | bytes 8454144 | tf_op jit(solution)/shard_map/all_gather | solution.py:34
  11.5 5.0 %copy-start.3 = (s32[8,2]{0,1:T(2,128)S(1)}, s32[8,2]{0,1:T(2,128)}, u32[]{:S(2)}) copy-start(s32[8,2]{0,1:T(2,128)} %param.10) | copy-start | bytes 196
  11.5 42.6 %all-to-all-start = ((bf16[4,8,64,896]{3,2,1,0:T(8,128)(2,1)}), bf16[4,8,64,896]{3,2,1,0:T(8,128)(2,1)}, u32[]{:S(2)}, u32[]{:S(2)}) async-start(bf16[4,8,64,896]{3,2,1,0:T(8,128)(2,1)} %broadcast_in_dim.47), calls=%async_computation | async-start | bytes 7340032 | tf_op jit(solution)/shard_map/all_to_all | solution.py:19
  61.3 54.4 %copy-start.4 = (f32[1024]{0:T(1024)S(1)}, f32[1024]{0:T(1024)}, u32[]{:S(2)}) copy-start(f32[1024]{0:T(1024)} %param.13) | copy-start | bytes 12292
  61.3 54.4 %copy-start.5 = (f32[1024]{0:T(1024)S(1)}, f32[1024]{0:T(1024)}, u32[]{:S(2)}) copy-start(f32[1024]{0:T(1024)} %param.12) | copy-start | bytes 12292
  115.7 8.4 %copy-start = (s32[8,64]{1,0:T(8,128)S(1)}, s32[8,64]{1,0:T(8,128)}, u32[]{:S(2)}) copy-start(s32[8,64]{1,0:T(8,128)} %param.8) | copy-start | bytes 6148
  115.7 51.0 %copy-start.1 = (s32[8,64]{1,0:T(8,128)S(1)}, s32[8,64]{1,0:T(8,128)}, u32[]{:S(2)}) copy-start(s32[8,64]{1,0:T(8,128)} %param.9) | copy-start | bytes 6148
  166.8 1.3 copy-start.2
Sparse Core Ops, SparseCore 0:
  11.1 93.6 all-gather.2
where the time goes:
time: 176 us; the launch traced here: 175 us
  waiting for transfers between devices  81.7 us (46%)
  blocking collectives  42.3 us (24%)
  local copies, waits for them, and re-layouts  21.9 us (12%)
  between operations  14.1 us (8%)
  matrix products  8.25 us (5%)
  starting transfers between devices  5 us (3%)
    all_gather x1, waiting for transfers between devices, score_rows(): lax.all_gather(w_first, SEQ, axis=0, tiled=True)  43.5 us
    psum x4, blocking collectives, over_axes(): shard = lax.psum(shard, axis)  42.3 us
    all_to_all x1, waiting for transfers between devices, sent_to_all(): return lax.all_to_all(copies, axis, split_axis=0, concat_axis=0, tiled=True)  37.6 us
    unnamed x14, local copies, waits for them, and re-layouts  13.4 us
    dot_general x1, matrix products, score_rows(): jnp.dot(rows, lax.all_gather(w_first, SEQ, axis=0, tiled=True), preferred...  8.25 us
    all_to_all x1, starting transfers between devices, sent_to_all(): return lax.all_to_all(copies, axis, split_axis=0, concat_axis=0, tiled=True)  4.96 us
    transpose x1, local copies, waits for them, and re-layouts, laid_out(): pieces = jnp.moveaxis(pieces, 0, dim)  4.88 us
    broadcast_in_dim x1, local copies, waits for them, and re-layouts, sent_to_all(): copies = jnp.broadcast_to(shard, (lax.axis_size(axis), *shard.shape))  3.55 us
  transfers between devices with their start and end apart: 2, of which 2 were waited for; matrix products, arithmetic and copies ran while one was open for 6% of the time, Pallas kernels for 0%

commit v1 on v0

--- a/solution.py
+++ b/solution.py
@@ -1,3 +1,4 @@
+import functools
 import jax
 import jax.numpy as jnp
 from jax import lax
@@ -6,6 +7,15 @@
 
 SEQ = ("seq_0", "seq_1", "seq_2")
 SEQ_HEAD = ("seq_0", "seq_1", "seq_2", "head")
+
+
+def switch_the_seats_all(inputs, lane_axis):
+    outer = jnp.stack(lax.axis_size(lane_axis) * [inputs])
+    h_now = jnp.concatenate(lax.all_to_all(outer, lane_axis, 0, 0), axis=0)
+    return h_now
+
+
+_render_teams = functools.partial(switch_the_seats_all, lane_axis=SEQ)
 
 
 def laid_out(pieces, dim):
@@ -30,9 +40,7 @@
 
 
 def score_rows(rows, w_first, b_first, w_second):
-    pre = jnp.dot(
-        rows, lax.all_gather(w_first, SEQ, axis=0, tiled=True), preferred_element_type=jnp.float32
-    )
+    pre = jnp.dot(rows, _render_teams(w_first), preferred_element_type=jnp.float32)
     return jnp.sum(jnp.maximum(pre + b_first, 0.0) * w_second, axis=-1)
 
 

time: 176 us -> 403 us (2.29)
  waiting for transfers between devices: 81.7 us -> 218 us
  blocking collectives: 42.3 us -> 125 us
  starting transfers between devices: 5 us -> 23.8 us
  between operations: 14.1 us -> 0.72 us
    all_to_all x1, waiting for transfers between devices: 37.6 us -> 218 us  [switch_the_seats_all(): h_now = jnp.concatenate(lax.all_to_all(outer, lane_axis, 0, 0), axis=0)]
    all_gather x1 -> x0, waiting for transfers between devices: 43.5 us -> none  [score_rows(): lax.all_gather(w_first, SEQ, axis=0, tiled=True)]
    all_to_all x0 -> x1, blocking collectives: none -> 42.7 us  [sent_to_all(): return lax.all_to_all(copies, axis, split_axis=0, concat_axis=0, tiled=True)]
    psum x4, blocking collectives: 42.3 us -> 82.1 us  [over_axes(): shard = lax.psum(shard, axis)]
    all_to_all x1, starting transfers between devices: 4.96 us -> 23.8 us  [switch_the_seats_all(): h_now = jnp.concatenate(lax.all_to_all(outer, lane_axis, 0, 0), axis=0)]
    unnamed x14 -> x15, local copies, waits for them, and re-layouts: 13.4 us -> 2.42 us
    reshape x0 -> x1, local copies, waits for them, and re-layouts: none -> 10.9 us  [switch_the_seats_all(): h_now = jnp.concatenate(lax.all_to_all(outer, lane_axis, 0, 0), axis=0)]
    another operation x0 -> x1, local copies, waits for them, and re-layouts: none -> 4.28 us  [switch_the_seats_all(): outer = jnp.stack(lax.axis_size(lane_axis) * [inputs])]
  transfers between devices with their start and end apart: 2 -> 1, of which waited for: 2 -> 1; matrix products, arithmetic and copies ran while one was open for 6% -> 2% of each run, Pallas kernels for 0% -> 0%
where the time goes in v1:
time: 403 us; the launch traced here: 402 us
  waiting for transfers between devices  218 us (54%)
  blocking collectives  125 us (31%)
  local copies, waits for them, and re-layouts  24.3 us (6%)
  starting transfers between devices  23.8 us (6%)
  matrix products  8.25 us (2%)
    all_to_all x1, waiting for transfers between devices, switch_the_seats_all(): h_now = jnp.concatenate(lax.all_to_all(outer, lane_axis, 0, 0), axis=0)  218 us
    psum x4, blocking collectives, over_axes(): shard = lax.psum(shard, axis)  82.1 us
    all_to_all x1, blocking collectives, sent_to_all(): return lax.all_to_all(copies, axis, split_axis=0, concat_axis=0, tiled=True)  42.7 us
    all_to_all x1, starting transfers between devices, switch_the_seats_all(): h_now = jnp.concatenate(lax.all_to_all(outer, lane_axis, 0, 0), axis=0)  23.8 us
    reshape x1, local copies, waits for them, and re-layouts, switch_the_seats_all(): h_now = jnp.concatenate(lax.all_to_all(outer, lane_axis, 0, 0), axis=0)  10.9 us
    dot_general x1, matrix products, score_rows(): jnp.dot(rows, _render_teams(w_first), preferred_element_type=jnp.float32)  8.25 us
  transfers between devices with their start and end apart: 1, of which 1 were waited for; matrix products, arithmetic and copies ran while one was open for 2% of the time, Pallas kernels for 0%

profile of v1, /device:TPU:1, one launch (start us, length us, event | category | flops | bytes accessed | tf_op | source)
XLA Modules:
  0.0 401.7 jit_solution(3544520017725640468)
XLA Ops:
  0.6 1.7 broadcast_in_dim.47
  2.3 0.0 copy-start
  2.3 42.7 %all_to_all.10 = bf16[4,8,64,896]{3,2,1,0:T(8,128)(2,1)} all-to-all(bf16[4,8,64,896]{3,2,1,0:T(8,128)(2,1)S(1)} %broadcast_in_dim.47), channel_id=1, replica_groups=mesh['seq_0'=8,'seq_1'=8,'seq_2'=2,'head'=4] {'head'}, dimensions={0} | all-to-all | bytes 7340032 | tf_op jit(solution)/shard_map/all_to_all | solution.py:29
  45.0 0.0 copy-done
  45.0 4.3 %stack.2 = bf16[128,28,1024]{2,1,0:T(8,128)(2,1)} broadcast(bf16[28,1024]{1,0:T(8,128)(2,1)S(1)} %copy-done), dimensions={1,2} | broadcast | bytes 7397376 | tf_op jit(solution)/shard_map/stack | solution.py:13
  49.3 0.0 copy-start.4
  49.3 23.8 %all-to-all-start.1 = ((bf16[128,28,1024]{2,1,0:T(8,128)(2,1)}), bf16[128,28,1024]{2,1,0:T(8,128)(2,1)}, u32[]{:S(2)}, u32[]{:S(2)}) async-start(bf16[128,28,1024]{2,1,0:T(8,128)(2,1)} %stack.2), calls=%async_computation.1 | async-start | bytes 16777216 | tf_op jit(solution)/shard_map/all_to_all | solution.py:14
  73.2 0.0 copy-done.4
  73.2 4.9 %copy.11 = bf16[8,64,4,896]{3,2,1,0:T(4,128)(2,1)S(1)} copy(bf16[8,64,4,896]{3,1,0,2:T(8,128)(2,1)} %bitcast.10) | data formatting | bytes 7340032 | tf_op jit(solution)/shard_map/transpose | solution.py:22
  78.1 2.4 copy.12
  80.5 0.0 copy-start.5
  80.5 0.0 copy-start.6
  80.5 218.1 %all-to-all-done.1 = bf16[128,28,1024]{2,1,0:T(8,128)(2,1)} async-done(((bf16[128,28,1024]{2,1,0:T(8,128)(2,1)}), bf16[128,28,1024]{2,1,0:T(8,128)(2,1)}, u32[]{:S(2)}, u32[]{:S(2)}) %all-to-all-start.1) | async-done | bytes 7340064 | tf_op jit(solution)/shard_map/all_to_all | solution.py:14
  298.5 10.9 %reshape.20 = bf16[3584,1024]{1,0:T(8,128)(2,1)} reshape(bf16[128,28,1024]{2,1,0:T(8,128)(2,1)} %all-to-all-done.1) | data formatting | bytes 14680064 | tf_op jit(solution)/shard_map/reshape | solution.py:14
  309.5 0.0 copy-done.5
  309.5 0.0 copy-done.6
  309.5 0.0 copy-start.1
  309.5 0.0 copy-start.2
  309.5 8.3 %multiply_reduce_fusion = f32[512]{0:T(512)S(1)} fusion(bf16[512,3584]{1,0:T(8,128)(2,1)} %bitcast.12, bf16[3584,1024]{1,0:T(8,128)(2,1)} %reshape.20, f32[1024]{0:T(1024)S(1)} %copy-done.5, f32[1024]{0:T(1024)S(1)} %copy-done.6), kind=kOutput, calls=%fused_computation | convolution fusion | flops 3760193024 | bytes 11020288 | tf_op jit(solution)/shard_map/dot_general | solution.py:43
  317.8 0.1 broadcast_in_dim.48
  317.8 0.0 copy-done.1
  317.8 0.3 select_reduce_fusion
  318.1 42.8 %psum.28 = f32[8,64]{1,0:T(8,128)S(1)} all-reduce(f32[8,64]{1,0:T(8,128)S(1)} %select_reduce_fusion), channel_id=1, replica_groups=mesh['seq_0'=8,'seq_1'=8,'seq_2'=2,'head'=4] {'seq_0'}, use_global_device_ids=true, to_apply=%region_2.3 | all-reduce | flops 512 | bytes 4096 | tf_op jit(solution)/shard_map/psum | solution.py:38
  360.9 22.4 %psum.29 = f32[8,64]{1,0:T(8,128)S(1)} all-reduce(f32[8,64]{1,0:T(8,128)S(1)} %psum.28), channel_id=1, replica_groups=mesh['seq_0'=8,'seq_1'=8,'seq_2'=2,'head'=4] {'seq_1'}, use_global_device_ids=true, to_apply=%region_3.4 | all-reduce | flops 512 | bytes 4096 | tf_op jit(solution)/shard_map/psum | solution.py:38
  383.3 10.1 %psum.30 = f32[8,64]{1,0:T(8,128)S(1)} all-reduce(f32[8,64]{1,0:T(8,128)S(1)} %psum.29), channel_id=1, replica_groups=mesh['seq_0'=8,'seq_1'=8,'seq_2'=2,'head'=4] {'seq_2'}, use_global_device_ids=true, to_apply=%region_4.5 | all-reduce | flops 512 | bytes 4096 | tf_op jit(solution)/shard_map/psum | solution.py:38
  393.4 6.8 %psum.31 = f32[8,64]{1,0:T(8,128)S(1)} all-reduce(f32[8,64]{1,0:T(8,128)S(1)} %psum.30), channel_id=1, replica_groups=mesh['seq_0'=8,'seq_1'=8,'seq_2'=2,'head'=4] {'head'}, use_global_device_ids=true, to_apply=%region_5.6 | all-reduce | flops 512 | bytes 4096 | tf_op jit(solution)/shard_map/psum | solution.py:38
  400.3 0.0 copy-done.2
  400.3 0.1 select_reduce_fusion.3
  400.4 0.0 copy-start.3
  400.4 0.6 broadcast_select_fusion
  401.0 0.2 select_reduce_fusion.1
  401.2 0.5 sub.3
  401.7 0.0 copy-done.3
  (2 shorter events, 0.0 us)
Async XLA Ops:
  2.3 42.7 %copy-start = (bf16[28,1024]{1,0:T(8,128)(2,1)S(1)}, bf16[28,1024]{1,0:T(8,128)(2,1)}, u32[]{:S(2)}) copy-start(bf16[28,1024]{1,0:T(8,128)(2,1)} %param.11) | copy-start | bytes 172036
  49.3 23.9 %copy-start.4 = (s32[8,2]{0,1:T(2,128)S(1)}, s32[8,2]{0,1:T(2,128)}, u32[]{:S(2)}) copy-start(s32[8,2]{0,1:T(2,128)} %param.10) | copy-start | bytes 196
  49.3 249.2 %all-to-all-start.1 = ((bf16[128,28,1024]{2,1,0:T(8,128)(2,1)}), bf16[128,28,1024]{2,1,0:T(8,128)(2,1)}, u32[]{:S(2)}, u32[]{:S(2)}) async-start(bf16[128,28,1024]{2,1,0:T(8,128)(2,1)} %stack.2), calls=%async_computation.1 | async-start | bytes 16777216 | tf_op jit(solution)/shard_map/all_to_all | solution.py:14
  80.5 229.0 %copy-start.5 = (f32[1024]{0:T(1024)S(1)}, f32[1024]{0:T(1024)}, u32[]{:S(2)}) copy-start(f32[1024]{0:T(1024)} %param.13) | copy-start | bytes 12292
  80.5 229.0 %copy-start.6 = (f32[1024]{0:T(1024)S(1)}, f32[1024]{0:T(1024)}, u32[]{:S(2)}) copy-start(f32[1024]{0:T(1024)} %param.12) | copy-start | bytes 12292
  309.5 8.4 %copy-start.1 = (s32[8,64]{1,0:T(8,128)S(1)}, s32[8,64]{1,0:T(8,128)}, u32[]{:S(2)}) copy-start(s32[8,64]{1,0:T(8,128)} %param.8) | copy-start | bytes 6148
  309.5 90.8 %copy-start.2 = (s32[8,64]{1,0:T(8,128)S(1)}, s32[8,64]{1,0:T(8,128)}, u32[]{:S(2)}) copy-start(s32[8,64]{1,0:T(8,128)} %param.9) | copy-start | bytes 6148
  400.4 1.3 copy-start.3
